TPU v7x, 32 devices: a whole 2x2x4 slice. The times are simulated.
32 devices in a mesh: terms: 2 (over x), rows: 4 (over y, core), cols: 4 (over z).
Axes of the slice: x: 2, y: 2, z: 4, core: 2. Of those that a mesh axis runs over, the one named last changes fastest.
Arguments:
- wavefunction: bfloat16 [2, 1024, 1024], P(None, 'rows', 'cols'), may hold values from -6 to 6
- energy: float32 [2], replicated, may hold values from 1 to 4
- block_rows: int32 [2], replicated, may hold values from 512 to 1024
- block_cols: int32 [2], replicated, may hold values from 512 to 1024
- left_ops: bfloat16 [8, 1024, 1024], P('terms', 'rows'), may hold values from -0.1875 to 0.1875
- right_ops: bfloat16 [8, 1024, 1024], P('terms', 'cols'), may hold values from -0.1875 to 0.1875
- source: int32 [8], P('terms'), may hold values from 0 to 1
- target: int32 [8], P('terms'), may hold values from 0 to 1
Outputs:
- sigma: bfloat16 [2, 1024, 1024], P(None, 'rows', 'cols')
- residual: bfloat16 [2, 1024, 1024], P(None, 'rows', 'cols')
Inputs may be any that keep to these rules, and one draw needn't show every extreme that they name: source[t] is the sector whose block term t reads. target[t] is the sector to which term t adds. `block_rows`: entries of a sector block beyond its live left or right states are ignored.
All inputs are finite; a program needn't handle non-finite values.
Results may differ from a plain program's by a relative error of at most 0.0044.
The roundings to bfloat16 on the way count: a program that leaves them out, or rounds other values in their place, can miss the bound.
Values may be sent and summed in bfloat16 or wider, within the bound.
No kernel may reach another device: no remote copies, remote signals or barrier semaphores. Data moves between devices by JAX's collectives and lax.ppermute only.
A program may use at most 64 MiB of HBM per device.

v0:
```python
import jax
import jax.numpy as jnp
from jax import lax
from jax.sharding import PartitionSpec as P

EPSILON = 1e-06


def per_device(wavefunction, energy, block_rows, block_cols, left_ops, right_ops, source, target):
    sectors, tile_rows, tile_cols = wavefunction.shape
    term_count = left_ops.shape[0]
    row_ids = lax.axis_index("rows") * tile_rows + lax.iota(jnp.int32, tile_rows)
    col_ids = lax.axis_index("cols") * tile_cols + lax.iota(jnp.int32, tile_cols)
    inside = (row_ids[None, :, None] < block_rows[:, None, None]) & (
        col_ids[None, None, :] < block_cols[:, None, None]
    )
    live_psi = jnp.where(inside, wavefunction, jnp.zeros_like(wavefunction))
    sector_ids = lax.iota(jnp.int32, sectors)
    partial_value = jnp.zeros((sectors, tile_rows, tile_cols), jnp.float32)
    panels = lax.all_gather(live_psi, "rows", axis=1, tiled=True)
    product_list = []
    for term_index in range(term_count):
        col_panel = lax.dynamic_index_in_dim(panels, source[term_index], 0, keepdims=False)
        product_list.append(
            jnp.dot(left_ops[term_index], col_panel, preferred_element_type=jnp.float32).astype(
                jnp.bfloat16
            )
        )
    products = jnp.stack(product_list)
    additions = jnp.einsum(
        "txl,tml->txm",
        lax.all_gather(products, "cols", axis=2, tiled=True),
        right_ops,
        preferred_element_type=jnp.float32,
    )
    for term_index in range(term_count):
        hit = (sector_ids == target[term_index])[:, None, None]
        partial_value = partial_value + jnp.where(hit, additions[term_index][None], 0.0)
    live_f = live_psi.astype(jnp.float32)
    summed = lax.psum(partial_value, "terms")
    full_sigma = jnp.where(inside, summed + energy[:, None, None] * live_f, 0.0)
    numerator, denominator = lax.psum(
        (jnp.sum(live_f * full_sigma), jnp.sum(live_f * live_f)), ("rows", "cols")
    )
    rayleigh = numerator / (denominator + EPSILON)
    residual = full_sigma - rayleigh * live_f
    return (full_sigma.astype(jnp.bfloat16), residual.astype(jnp.bfloat16))


def solution(mesh):
    in_specs = (
        P(None, "rows", "cols"),
        P(),
        P(),
        P(),
        P("terms", "rows", None),
        P("terms", "cols", None),
        P("terms"),
        P("terms"),
    )
    out_specs = (P(None, "rows", "cols"), P(None, "rows", "cols"))
    return jax.shard_map(
        per_device, mesh=mesh, in_specs=in_specs, out_specs=out_specs, check_vma=False
    )
```

profile of v0, /device:TPU:0, one launch (start us, length us, event | category | flops | bytes accessed | tf_op | source)
XLA Modules:
  0.0 158.2 jit_solution(4470335550946866538)
XLA Ops:
  7.2 0.0 copy-start
  7.2 0.0 all-gather.3.cloned.1.call-start
  7.3 0.9 broadcast_compare_fusion
  8.1 1.8 %and_select_fusion.1 = bf16[2,256,256]{2,1,0:T(8,128)(2,1)} fusion(bf16[2,256,256]{2,1,0:T(8,128)(2,1)} %param.8, pred[2,256]{1,0:T(4,128)(4,1)S(1)} %get-tuple-element.20, pred[2,256]{1,0:T(4,128)(4,1)S(1)} %get-tuple-element.21), kind=kLoop, calls=%fused_computation.13 | loop fusion | flops 262144 | bytes 525312 | tf_op jit(solution)/shard_map/jit(_where)/select_n | solution.py:17
  9.9 0.0 all-gather.3.cloned.1.call-update
  10.0 0.0 all-gather.5.cloned.1.call-start
  10.0 1.5 fusion.31
  19.3 10.4 %all-gather.3.cloned.1.call-done = bf16[2,1024,256]{2,1,0:T(8,128)(2,1)} async-done(((bf16[2,256,256]{2,1,0:T(8,128)(2,1)}), bf16[2,1024,256]{2,1,0:T(8,128)(2,1)}) %all-gather.3.cloned.1.call-update) | async-done | bytes 1048592 | tf_op jit(solution)/shard_map/all_gather | solution.py:20
  29.6 0.0 copy-start.4
  29.6 0.0 copy-start.5
  29.6 1.7 %fusion = bf16[1,256,256]{1,2,0:T(8,128)(2,1)S(1)} fusion(bf16[4,256,1024]{2,1,0:T(8,128)(2,1)} %param.12, bf16[2,1024,256]{2,1,0:T(8,128)(2,1)} %all-gather.3.cloned.1.call-done, s32[]{:T(128)S(6)} %select_n.35), kind=kOutput, calls=%fused_computation.4 | convolution fusion | flops 134283264 | bytes 1179652 | tf_op jit(solution)/shard_map/dot_general | solution.py:25
  31.3 1.6 fusion.1
  32.9 0.0 copy-done.4
  32.9 0.0 copy-start.2
  32.9 1.4 fusion.2
  34.3 0.0 copy-done.5
  34.3 0.4 fusion.3
  34.7 0.9 pad_maximum_fusion
  35.6 0.0 all-gather.5.cloned.1.call-update
  35.6 0.0 all-reduce.3.cloned.1.call-start
  35.6 0.0 copy-done.2
  35.7 0.6 fusion.30
  36.2 1.1 iota_compare_fusion
  37.4 1.3 iota_compare_fusion.2
  38.7 42.7 %all-gather.5.cloned.1.call-done = bf16[4,256,1024]{1,2,0:T(8,128)(2,1)} async-done(((bf16[4,256,256]{1,2,0:T(8,128)(2,1)}), bf16[4,256,1024]{1,2,0:T(8,128)(2,1)}) %all-gather.5.cloned.1.call-update) | async-done | bytes 2097168 | tf_op jit(solution)/shard_map/all_gather | solution.py:32
  81.4 0.0 copy-done
  81.4 2.4 %fusion.32 = f32[4,256,256]{2,1,0:T(8,128)S(1)} fusion(bf16[4,256,1024]{1,2,0:T(8,128)(2,1)} %all-gather.5.cloned.1.call-done, bf16[4,256,1024]{2,1,0:T(8,128)(2,1)S(1)} %copy-done), kind=kOutput, calls=%fused_computation.56 | convolution fusion | flops 536870912 | bytes 5242880 | tf_op jit(solution)/shard_map/txl,tml->txm/dot_general | solution.py:30
  83.9 0.0 copy-start.1
  83.9 0.0 copy-start.3
  83.9 0.1 slice_bitcast_fusion.3
  84.0 1.0 select_add_fusion
  85.0 0.0 all-reduce.3.cloned.1.call-update
  85.0 27.6 %all-reduce.3.cloned.1.call-done = f32[2,256,256]{2,1,0:T(8,128)} async-done(((f32[2,256,256]{2,1,0:T(8,128)}), f32[2,256,256]{2,1,0:T(8,128)}) %all-reduce.3.cloned.1.call-update) | async-done | bytes 524304 | tf_op jit(solution)/shard_map/psum | solution.py:40
  112.6 0.0 copy-done.1
  112.6 0.0 copy-done.3
  112.6 2.0 %fusion.6 = (f32[]{:T(128)}, f32[]{:T(128)}) fusion(f32[2,256,256]{2,1,0:T(8,128)} %all-reduce.3.cloned.1.call-done, f32[2]{0:T(128)S(1)} %copy-done.3, pred[2,256]{1,0:T(4,128)(4,1)S(1)} %get-tuple-element.20, pred[2,256]{1,0:T(4,128)(4,1)S(1)} %get-tuple-element.21, bf16[2,256,256]{2,1,0:T(8,128)(2,1)S(1)} %copy-done.1), kind=kLoop, calls=%fused_computation.16 | loop fusion | flops 1310718 | bytes 787472 | tf_op jit(solution)/shard_map/reduce_sum | solution.py:43
  114.6 33.8 %all-reduce = (f32[]{:T(128)}, f32[]{:T(128)}) all-reduce(f32[]{:T(128)} %get-tuple-element.3, f32[]{:T(128)} %get-tuple-element.2), channel_id=1, replica_groups=mesh['terms'=2,'rows'=4,'cols'=4] {'rows','cols'}, use_global_device_ids=true, to_apply=%region_2.3 | all-reduce | flops 2 | bytes 16 | tf_op jit(solution)/shard_map/psum | solution.py:42
  149.6 2.1 %fusion.8 = (bf16[2,256,256]{2,1,0:T(8,128)(2,1)}, bf16[2,256,256]{2,1,0:T(8,128)(2,1)}) fusion(f32[]{:T(128)S(6)} %div.3, f32[2,256,256]{2,1,0:T(8,128)} %all-reduce.3.cloned.1.call-done, f32[2]{0:T(128)S(1)} %copy-done.3, pred[2,256]{1,0:T(4,128)(4,1)S(1)} %get-tuple-element.20, pred[2,256]{1,0:T(4,128)(4,1)S(1)} %get-tuple-element.21, ...), kind=kLoop, calls=%fused_computation.18 | loop fusion | flops 1310720 | bytes 1311756 | tf_op jit(solution)/shard_map/convert_element_type | solution.py:47
  (2 shorter events, 0.0 us)
Async XLA Ops:
  7.2 74.2 %copy-start = (bf16[4,256,1024]{2,1,0:T(8,128)(2,1)S(1)}, bf16[4,256,1024]{2,1,0:T(8,128)(2,1)}, u32[]{:S(2)}) copy-start(bf16[4,256,1024]{2,1,0:T(8,128)(2,1)} %param.13) | copy-start | bytes 6291460
  7.2 22.4 %all-gather.3.cloned.1.call-start = ((), (), s32[]{:S(2)}) async-start(), calls=%async_computation | async-start | bytes 1310720 | tf_op jit(solution)/shard_map/all_gather | solution.py:20
  10.0 71.4 %all-gather.5.cloned.1.call-start = ((), (), s32[]{:S(2)}) async-start(), calls=%async_computation.1 | async-start | bytes 2621440 | tf_op jit(solution)/shard_map/all_gather | solution.py:32
  29.6 3.3 %copy-start.4 = (bf16[4,256,1024]{2,1,0:T(8,128)(2,1)S(1)}, bf16[4,256,1024]{2,1,0:T(8,128)(2,1)}, u32[]{:S(2)}) copy-start(bf16[4,256,1024]{2,1,0:T(8,128)(2,1)} %param.12) | copy-start | bytes 6291460
  29.6 4.7 %copy-start.5 = (bf16[2,1024,256]{2,1,0:T(8,128)(2,1)S(1)}, bf16[2,1024,256]{2,1,0:T(8,128)(2,1)}, u32[]{:S(2)}) copy-start(bf16[2,1024,256]{2,1,0:T(8,128)(2,1)} %all-gather.3.cloned.1.call-done) | copy-start | bytes 3145732
  32.9 2.7 %copy-start.2 = (s32[4]{0:T(128)S(1)}, s32[4]{0:T(128)}, u32[]{:S(2)}) copy-start(s32[4]{0:T(128)} %param.15) | copy-start | bytes 52
  35.6 77.0 %all-reduce.3.cloned.1.call-start = ((), (), s32[]{:S(2)}) async-start(), calls=%async_computation.2 | async-start | bytes 1048576 | tf_op jit(solution)/shard_map/psum | solution.py:40
  83.9 28.7 %copy-start.1 = (bf16[2,256,256]{2,1,0:T(8,128)(2,1)S(1)}, bf16[2,256,256]{2,1,0:T(8,128)(2,1)}, u32[]{:S(2)}) copy-start(bf16[2,256,256]{2,1,0:T(8,128)(2,1)} %param.8) | copy-start | bytes 786436
  83.9 28.7 %copy-start.3 = (f32[2]{0:T(128)S(1)}, f32[2]{0:T(128)}, u32[]{:S(2)}) copy-start(f32[2]{0:T(128)} %param.9) | copy-start | bytes 28
Sparse Core Ops, SparseCore 0:
  10.1 19.4 all-gather.2
  35.7 45.6 all-gather.4
  85.1 27.4 all-reduce.2
where the time goes:
time: 159 us; the launch traced here: 158 us
  waiting for transfers between devices  80.8 us (51%)
  blocking collectives  33.8 us (21%)
  between operations  23 us (14%)
  other arithmetic  11 us (7%)
  matrix products  7.45 us (5%)
  local copies, waits for them, and re-layouts  2.17 us (1%)
    all_gather x1, waiting for transfers between devices, per_device(): lax.all_gather(products, 'cols', axis=2, tiled=True)  42.7 us
    psum x1, blocking collectives, per_device(): lax.psum((jnp.sum(live_f * full_sigma), jnp.sum(live_f * live_f)), ('rows...  33.8 us
    psum x1, waiting for transfers between devices, per_device(): summed = lax.psum(partial_value, 'terms')  27.6 us
    all_gather x1, waiting for transfers between devices, per_device(): panels = lax.all_gather(live_psi, 'rows', axis=1, tiled=True)  10.4 us
    dot_general x4, matrix products, per_device(): jnp.dot(left_ops[term_index], col_panel, preferred_element_type=jnp.float32)  5 us
  transfers between devices with their start and end apart: 3, of which 3 were waited for; matrix products, arithmetic and copies ran while one was open for 3% of the time, Pallas kernels for 0%

commit v1 on v0

v1 whole, which is shorter than its diff:
```python
import functools

import jax
import jax.numpy as jnp
from jax import lax
from jax.experimental import pallas as pl
from jax.experimental.pallas import tpu as pltpu
from jax.sharding import PartitionSpec as P

EPSILON = 1e-06
F32 = jnp.float32
BF16 = jnp.bfloat16
VMEM = pl.BlockSpec(memory_space=pltpu.VMEM)
SMEM = pl.BlockSpec(memory_space=pltpu.SMEM)


def swap(value, axis, size, bit):
    return lax.ppermute(value, axis, [(i, i ^ bit) for i in range(size)])


def shift(value, axis, size, step):
    return lax.ppermute(value, axis, [(i, (i + step) % size) for i in range(size)])


def masked(block, rows_left, cols_left):
    rows, cols = block.shape
    inside = (lax.broadcasted_iota(jnp.int32, (rows, cols), 0) < rows_left) & (
        lax.broadcasted_iota(jnp.int32, (rows, cols), 1) < cols_left
    )
    return jnp.where(inside, block.astype(F32), 0.0)


def right_kernel(cols_n, source, block_rows, block_cols, own, *refs):
    steps = cols_n - 1
    near, far = refs[:steps], refs[steps : 2 * steps]
    right, out, panel = refs[2 * steps :]
    sectors, rows, cols = own.shape
    row0 = lax.axis_index("rows") * rows
    me = lax.axis_index("cols")
    mine = lax.rem(lax.axis_index("terms"), 2)
    for s in range(sectors):
        panel[s, :, pl.ds(pl.multiple_of(me * cols, cols), cols)] = masked(
            own[s], block_rows[s] - row0, block_cols[s] - me * cols
        ).astype(BF16)
    for k in range(1, cols_n):
        at = lax.rem(me - k + cols_n, cols_n)
        for ref, s in ((near[k - 1], mine), (far[k - 1], 1 - mine)):
            panel[s, :, pl.ds(pl.multiple_of(at * cols, cols), cols)] = masked(
                ref[...], block_rows[s] - row0, block_cols[s] - at * cols
            ).astype(BF16)
    for t in range(right.shape[0]):
        out[t] = lax.dot_general(
            panel[source[t]], right[t], (((1,), (1,)), ((), ())), preferred_element_type=F32
        ).astype(BF16)


def left_kernel(rows_n, target, block_rows, block_cols, energy, own, left, *refs):
    parts = refs[:rows_n]
    out, sums, acc = refs[rows_n:]
    sectors, rows, cols = own.shape
    me = lax.axis_index("rows")
    row0 = me * rows
    col0 = lax.axis_index("cols") * cols
    acc[...] = jnp.zeros_like(acc)
    for t in range(left.shape[0]):
        total = None
        for j in range(rows_n):
            at = pl.multiple_of((me ^ j) * rows, rows)
            part = jnp.dot(left[t, :, pl.ds(at, rows)], parts[j][t], preferred_element_type=F32)
            total = part if total is None else total + part
        acc[target[t]] += total
    upper = jnp.zeros((8, 128), F32)
    steady = jnp.zeros((8, 128), F32)
    lower = jnp.zeros((8, 128), F32)
    fold = lambda v: v.reshape(rows // 8, 8, cols // 128, 128).sum((0, 2))
    for s in range(sectors):
        share = acc[s].astype(BF16)
        out[s] = share
        live = masked(own[s], block_rows[s] - row0, block_cols[s] - col0)
        upper = upper + fold(live * share.astype(F32))
        square = fold(live * live)
        steady = steady + energy[s] * square
        lower = lower + square
    sums[0] = upper
    sums[1] = steady
    sums[2] = lower


def last_kernel(block_rows, block_cols, energy, own, here, there, sums, sigma, residual):
    sectors, rows, cols = own.shape
    row0 = lax.axis_index("rows") * rows
    col0 = lax.axis_index("cols") * cols
    rayleigh = (jnp.sum(sums[0]) + jnp.sum(sums[1])) / (jnp.sum(sums[2]) + EPSILON)
    for s in range(sectors):
        live = masked(own[s], block_rows[s] - row0, block_cols[s] - col0)
        full = masked(
            here[s].astype(F32) + there[s].astype(F32), block_rows[s] - row0, block_cols[s] - col0
        ) + energy[s] * live
        sigma[s] = full.astype(BF16)
        residual[s] = (full - rayleigh * live).astype(BF16)


def sum_rows_cols(value, rows_n, cols_n):
    for axis, size in (("rows", rows_n), ("cols", cols_n)):
        bit = 1
        while bit < size:
            value = value + swap(value, axis, size, bit)
            bit *= 2
    return value


def per_device(
    terms_n, rows_n, cols_n, wavefunction, energy, block_rows, block_cols, left, right, source, target
):
    sectors, rows, cols = wavefunction.shape
    terms = left.shape[0]
    mine = lax.rem(lax.axis_index("terms"), 2)
    half = lax.dynamic_index_in_dim(wavefunction, mine, 0, keepdims=False)
    near = [shift(half, "cols", cols_n, k) for k in range(1, cols_n)]
    far = [swap(block, "terms", terms_n, 1) for block in near]
    right_part = pl.pallas_call(
        functools.partial(right_kernel, cols_n),
        out_shape=jax.ShapeDtypeStruct((terms, rows, cols), BF16),
        in_specs=[SMEM] * 3 + [VMEM] * (2 * cols_n),
        out_specs=VMEM,
        scratch_shapes=[pltpu.VMEM((sectors, rows, cols * cols_n), BF16)],
    )(source, block_rows, block_cols, wavefunction, *near, *far, right)
    parts = {0: right_part}
    bit = rows_n // 2
    while bit:
        parts.update({j ^ bit: swap(v, "rows", rows_n, bit) for j, v in list(parts.items())})
        bit //= 2
    share, sums = pl.pallas_call(
        functools.partial(left_kernel, rows_n),
        out_shape=(
            jax.ShapeDtypeStruct((sectors, rows, cols), BF16),
            jax.ShapeDtypeStruct((3, 8, 128), F32),
        ),
        in_specs=[SMEM] * 4 + [VMEM] * (2 + rows_n),
        out_specs=(VMEM, VMEM),
        scratch_shapes=[pltpu.VMEM((sectors, rows, cols), F32)],
    )(target, block_rows, block_cols, energy, wavefunction, left, *[parts[j] for j in range(rows_n)])
    if terms_n == 2:
        others = swap(share, "terms", terms_n, 1)
        sums = sums.at[0].add(swap(sums[0], "terms", terms_n, 1))
    else:
        total = lax.psum(share.astype(F32), "terms")
        others = total - share.astype(F32)
        sums = sums.at[0].set(lax.psum(sums[0], "terms"))
    sums = sum_rows_cols(sums, rows_n, cols_n)
    return pl.pallas_call(
        last_kernel,
        out_shape=(jax.ShapeDtypeStruct((sectors, rows, cols), BF16),) * 2,
        in_specs=[SMEM] * 3 + [VMEM] * 4,
        out_specs=(VMEM, VMEM),
    )(block_rows, block_cols, energy, wavefunction, share, others, sums)


def solution(mesh):
    sizes = tuple(mesh.shape[a] for a in ("terms", "rows", "cols"))
    in_specs = (
        P(None, "rows", "cols"),
        P(),
        P(),
        P(),
        P("terms", "rows", None),
        P("terms", "cols", None),
        P("terms"),
        P("terms"),
    )
    out_specs = (P(None, "rows", "cols"), P(None, "rows", "cols"))
    return jax.shard_map(
        functools.partial(per_device, *sizes),
        mesh=mesh,
        in_specs=in_specs,
        out_specs=out_specs,
        check_vma=False,
    )
```

time: 159 us -> 73.5 us (0.46)
  waiting for transfers between devices: 80.8 us -> 40.7 us
  blocking collectives: 33.8 us -> 0 us
  between operations: 23 us -> 0.71 us
  starting transfers between devices: 0.12 us -> 14.8 us
  Pallas kernels: 0 us -> 10.7 us
  other arithmetic: 11 us -> 2.6 us
  matrix products: 7.45 us -> 0 us
  local copies, waits for them, and re-layouts: 2.17 us -> 3.77 us
    all_gather x2 -> x0, waiting for transfers between devices: 53.1 us -> none  [the longest x1 42.7 us: per_device(): lax.all_gather(products, 'cols', axis=2, tiled=True)]
    ppermute x0 -> x15, waiting for transfers between devices: none -> 40.7 us  [the longest x12 32 us: swap(): return lax.ppermute(value, axis, [(i, i ^ bit) for i in range(size)])]
    psum x1 -> x0, blocking collectives: 33.8 us -> none  [per_device(): lax.psum((jnp.sum(live_f * full_sigma), jnp.sum(live_f * live_f)), ('rows...]
    psum x1 -> x0, waiting for transfers between devices: 27.6 us -> none  [per_device(): summed = lax.psum(partial_value, 'terms')]
    ppermute x0 -> x15, starting transfers between devices: none -> 14.8 us  [the longest x12 8.61 us: swap(): return lax.ppermute(value, axis, [(i, i ^ bit) for i in range(size)])]
    pallas_call x0 -> x3, Pallas kernels: none -> 10.7 us  [the longest x1 4.46 us: per_device(): pl.pallas_call(functools.partial(left_kernel, rows_n), out_shape=(jax.Sha...]
    dot_general x5 -> x0, matrix products: 7.45 us -> none  [the longest x4 5 us: per_device(): jnp.dot(left_ops[term_index], col_panel, preferred_element_type=jnp.float32)]
    eq x2 -> x0, other arithmetic: 2.41 us -> none  [per_device(): hit = (sector_ids == target[term_index])[:, None, None]]
  transfers between devices with their start and end apart: 3 -> 15, of which waited for: 3 -> 11; matrix products, arithmetic and copies ran while one was open for 3% -> 4% of each run, Pallas kernels for 0% -> 0%
where the time goes in v1:
time: 73.5 us; the launch traced here: 73.2 us
  waiting for transfers between devices  40.7 us (55%)
  starting transfers between devices  14.8 us (20%)
  Pallas kernels  10.7 us (15%)
  local copies, waits for them, and re-layouts  3.77 us (5%)
  other arithmetic  2.6 us (4%)
    ppermute x12, waiting for transfers between devices, swap(): return lax.ppermute(value, axis, [(i, i ^ bit) for i in range(size)])  32 us
    ppermute x3, waiting for transfers between devices, shift(): lax.ppermute(value, axis, [(i, (i + step) % size) for i in range(size)])  8.71 us
    ppermute x12, starting transfers between devices, swap(): return lax.ppermute(value, axis, [(i, i ^ bit) for i in range(size)])  8.61 us
    ppermute x3, starting transfers between devices, shift(): lax.ppermute(value, axis, [(i, (i + step) % size) for i in range(size)])  6.14 us
    pallas_call x1, Pallas kernels, per_device(): pl.pallas_call(functools.partial(left_kernel, rows_n), out_shape=(jax.Sha...  4.46 us
    pallas_call x1, Pallas kernels, per_device(): pl.pallas_call(functools.partial(right_kernel, cols_n), out_shape=jax.Sha...  3.97 us
    pallas_call x1, Pallas kernels, per_device(): pl.pallas_call(last_kernel, out_shape=(jax.ShapeDtypeStruct((sectors, row...  2.32 us
    unnamed x20, local copies, waits for them, and re-layouts  2.17 us
  transfers between devices with their start and end apart: 15, of which 11 were waited for; matrix products, arithmetic and copies ran while one was open for 4% of the time, Pallas kernels for 0%

profile of v1, /device:TPU:0, one launch (start us, length us, event | category | flops | bytes accessed | tf_op | source)
XLA Modules:
  0.0 73.2 jit_solution(4326500344729016815)
XLA Ops:
  0.6 0.9 %dynamic-slice_bitcast_fusion = bf16[256,256]{1,0:T(8,128)(2,1)S(1)} fusion(bf16[2,256,256]{2,1,0:T(8,128)(2,1)} %own.5, s32[]{:T(128)S(6)} %select_n.4), kind=kLoop, calls=%fused_computation | loop fusion | bytes 262148 | tf_op jit(solution)/shard_map/jit(dynamic_index_in_dim)/squeeze | solution.py:118
  1.6 5.1 %collective-permute-start.2 = (bf16[256,256]{1,0:T(8,128)(2,1)S(1)}, bf16[256,256]{1,0:T(8,128)(2,1)S(1)}, u32[]{:S(2)}, u32[]{:S(2)}) collective-permute-start(bf16[256,256]{1,0:T(8,128)(2,1)S(1)} %dynamic-slice_bitcast_fusion), channel_id=1, source_target_pairs={{0,3},{1,0},{2,1},{3,2},{4,7},{5,4},{6,5},{7,6},{8,11},{9,8},{10,9... | collective-permute-start | bytes 393224 | tf_op jit(solution)/shard_map/ppermute | solution.py:22
  6.7 0.0 collective-permute-start.1
  6.7 1.0 %collective-permute-start = (bf16[256,256]{1,0:T(8,128)(2,1)S(1)}, bf16[256,256]{1,0:T(8,128)(2,1)S(1)}, u32[]{:S(2)}, u32[]{:S(2)}) collective-permute-start(bf16[256,256]{1,0:T(8,128)(2,1)S(1)} %dynamic-slice_bitcast_fusion), channel_id=1, source_target_pairs={{0,1},{1,2},{2,3},{3,0},{4,5},{5,6},{6,7},{7,4},{8,9},{9,10},{10,1... | collective-permute-start | bytes 393224 | tf_op jit(solution)/shard_map/ppermute | solution.py:22
  7.7 2.9 %collective-permute-done.2.refs_2_ = bf16[256,256]{1,0:T(8,128)(2,1)S(1)} collective-permute-done((bf16[256,256]{1,0:T(8,128)(2,1)S(1)}, bf16[256,256]{1,0:T(8,128)(2,1)S(1)}, u32[]{:S(2)}, u32[]{:S(2)}) %collective-permute-start.2) | collective-permute-done | bytes 131104 | tf_op jit(solution)/shard_map/ppermute | solution.py:22
  10.6 1.5 %collective-permute-start.5 = (bf16[256,256]{1,0:T(8,128)(2,1)S(1)}, bf16[256,256]{1,0:T(8,128)(2,1)S(1)}, u32[]{:S(2)}, u32[]{:S(2)}) collective-permute-start(bf16[256,256]{1,0:T(8,128)(2,1)S(1)} %collective-permute-done.2.refs_2_), channel_id=1, source_target_pairs={{0,16},{16,0},{1,17},{17,1},{2,18},{18,2},{3,19},{19,3},{4,20},{20... | collective-permute-start | bytes 393224 | tf_op jit(solution)/shard_map/ppermute | solution.py:18
  12.1 5.8 %collective-permute-done.1.refs_1_ = bf16[256,256]{1,0:T(8,128)(2,1)S(1)} collective-permute-done((bf16[256,256]{1,0:T(8,128)(2,1)S(1)}, bf16[256,256]{1,0:T(8,128)(2,1)S(1)}, u32[]{:S(2)}, u32[]{:S(2)}) %collective-permute-start.1) | collective-permute-done | bytes 131104 | tf_op jit(solution)/shard_map/ppermute | solution.py:22
  17.9 1.5 %collective-permute-start.4 = (bf16[256,256]{1,0:T(8,128)(2,1)S(1)}, bf16[256,256]{1,0:T(8,128)(2,1)S(1)}, u32[]{:S(2)}, u32[]{:S(2)}) collective-permute-start(bf16[256,256]{1,0:T(8,128)(2,1)S(1)} %collective-permute-done.1.refs_1_), channel_id=1, source_target_pairs={{0,16},{16,0},{1,17},{17,1},{2,18},{18,2},{3,19},{19,3},{4,20},{20... | collective-permute-start | bytes 393224 | tf_op jit(solution)/shard_map/ppermute | solution.py:18
  19.4 0.0 collective-permute-done.refs_0_
  19.4 0.5 collective-permute-start.3
  19.9 0.0 collective-permute-done.5.refs_5_
  19.9 4.2 %collective-permute-done.4.refs_4_ = bf16[256,256]{1,0:T(8,128)(2,1)S(1)} collective-permute-done((bf16[256,256]{1,0:T(8,128)(2,1)S(1)}, bf16[256,256]{1,0:T(8,128)(2,1)S(1)}, u32[]{:S(2)}, u32[]{:S(2)}) %collective-permute-start.4) | collective-permute-done | bytes 131104 | tf_op jit(solution)/shard_map/ppermute | solution.py:18
  24.1 1.4 %collective-permute-done.3.refs_3_ = bf16[256,256]{1,0:T(8,128)(2,1)S(1)} collective-permute-done((bf16[256,256]{1,0:T(8,128)(2,1)S(1)}, bf16[256,256]{1,0:T(8,128)(2,1)S(1)}, u32[]{:S(2)}, u32[]{:S(2)}) %collective-permute-start.3) | collective-permute-done | bytes 131104 | tf_op jit(solution)/shard_map/ppermute | solution.py:18
  25.5 0.0 copy-done.4
  25.5 0.0 copy-done.5
  25.5 0.0 copy-done.6
  25.5 0.0 copy-done.7
  25.5 0.0 copy-done.8
  25.6 0.0 copy-start.9
  25.6 0.6 copy-done.9
  26.2 4.0 %shard_map.95.refs_0_ = bf16[4,256,256]{2,1,0:T(8,128)(2,1)} custom-call(s32[4]{0:T(128)} %source.1, s32[2]{0:T(128)} %block_rows.5, s32[2]{0:T(128)} %block_cols.5, bf16[2,256,256]{2,1,0:T(8,128)(2,1)} %own.5, bf16[256,256]{1,0:T(8,128)(2,1)} %copy-done.6, bf16[256,256]{1,0:T(8,128)(2,1)} %copy-done.5, bf16[256,256]{1,0:T(8,128)(2,1)} %copy-done.4, ...), custom_call_target="tpu_custom_call" | custom-call | tf_op jit(solution)/shard_map/pallas_call | solution.py:121
  30.2 1.5 %collective-permute-start.7 = (bf16[4,256,256]{2,1,0:T(8,128)(2,1)}, bf16[4,256,256]{2,1,0:T(8,128)(2,1)S(1)}, u32[]{:S(2)}, u32[]{:S(2)}) collective-permute-start(bf16[4,256,256]{2,1,0:T(8,128)(2,1)} %shard_map.95.refs_0_), channel_id=1, source_target_pairs={{0,8},{4,12},{8,0},{12,4},{1,9},{5,13},{9,1},{13,5},{2,10},{6,14},... | collective-permute-start | bytes 1572872 | tf_op jit(solution)/shard_map/ppermute | solution.py:18
  31.7 0.0 collective-permute-start.6
  31.7 11.1 %collective-permute-done.7.refs_2_ = bf16[4,256,256]{2,1,0:T(8,128)(2,1)S(1)} collective-permute-done((bf16[4,256,256]{2,1,0:T(8,128)(2,1)}, bf16[4,256,256]{2,1,0:T(8,128)(2,1)S(1)}, u32[]{:S(2)}, u32[]{:S(2)}) %collective-permute-start.7) | collective-permute-done | bytes 524320 | tf_op jit(solution)/shard_map/ppermute | solution.py:18
  42.8 0.0 collective-permute-start.8
  42.8 0.0 collective-permute-done.6.refs_1_
  42.8 0.0 copy-start.1
  42.8 1.9 %collective-permute-done.8.refs_3_ = bf16[4,256,256]{2,1,0:T(8,128)(2,1)S(1)} collective-permute-done((bf16[4,256,256]{2,1,0:T(8,128)(2,1)S(1)}, bf16[4,256,256]{2,1,0:T(8,128)(2,1)S(1)}, u32[]{:S(2)}, u32[]{:S(2)}) %collective-permute-start.8) | collective-permute-done | bytes 524320 | tf_op jit(solution)/shard_map/ppermute | solution.py:18
  44.7 0.8 %copy-done.2 = bf16[4,256,256]{2,1,0:T(8,128)(2,1)} copy-done((bf16[4,256,256]{2,1,0:T(8,128)(2,1)}, bf16[4,256,256]{2,1,0:T(8,128)(2,1)S(1)}, u32[]{:S(2)}) %copy-start.2) | copy-done | bytes 524312
  45.5 4.5 %shard_map.96 = (bf16[2,256,256]{2,1,0:T(8,128)(2,1)}, f32[3,8,128]{2,1,0:T(8,128)}) custom-call(s32[4]{0:T(128)} %target.1, s32[2]{0:T(128)} %block_rows.5, s32[2]{0:T(128)} %block_cols.5, f32[2]{0:T(128)} %energy.3, bf16[2,256,256]{2,1,0:T(8,128)(2,1)} %own.5, bf16[4,256,1024]{2,1,0:T(8,128)(2,1)} %left.1, bf16[4,256,256]{2,1,0:T(8,128)(2,1)} %shard_map.95.refs_0_, ...), custom_call_target="tpu_custom_call" | custom-call | tf_op jit(solution)/shard_map/pallas_call | solution.py:133
  49.9 0.7 slice_bitcast_fusion
  50.6 1.5 %collective-permute-start.10 = (f32[8,128]{1,0:T(8,128)S(1)}, f32[8,128]{1,0:T(8,128)S(1)}, u32[]{:S(2)}, u32[]{:S(2)}) collective-permute-start(f32[8,128]{1,0:T(8,128)S(1)} %slice_bitcast_fusion), channel_id=1, source_target_pairs={{0,16},{16,0},{1,17},{17,1},{2,18},{18,2},{3,19},{19,3},{4,20},{20... | collective-permute-start | bytes 12296 | tf_op jit(solution)/shard_map/ppermute | solution.py:18
  52.1 0.5 collective-permute-start.9
  52.7 1.6 %collective-permute-done.10 = f32[8,128]{1,0:T(8,128)S(1)} collective-permute-done((f32[8,128]{1,0:T(8,128)S(1)}, f32[8,128]{1,0:T(8,128)S(1)}, u32[]{:S(2)}, u32[]{:S(2)}) %collective-permute-start.10) | collective-permute-done | bytes 4128 | tf_op jit(solution)/shard_map/ppermute | solution.py:18
  54.2 1.3 %fusion = f32[3,8,128]{2,1,0:T(8,128)} fusion(f32[3,8,128]{2,1,0:T(8,128)} %get-tuple-element.17, f32[8,128]{1,0:T(8,128)S(1)} %collective-permute-done.10), kind=kLoop, calls=%fused_computation.2 | loop fusion | flops 1024 | bytes 12288 | tf_op jit(solution)/shard_map/scatter-add | solution.py:145
  55.5 0.0 collective-permute-start.11
  55.5 1.4 %collective-permute-done.11 = f32[3,8,128]{2,1,0:T(8,128)S(1)} collective-permute-done((f32[3,8,128]{2,1,0:T(8,128)}, f32[3,8,128]{2,1,0:T(8,128)S(1)}, u32[]{:S(2)}, u32[]{:S(2)}) %collective-permute-start.11) | collective-permute-done | bytes 12320 | tf_op jit(solution)/shard_map/ppermute | solution.py:18
  56.9 0.7 add.25
  57.6 1.5 %collective-permute-start.12 = (f32[3,8,128]{2,1,0:T(8,128)S(1)}, f32[3,8,128]{2,1,0:T(8,128)S(1)}, u32[]{:S(2)}, u32[]{:S(2)}) collective-permute-start(f32[3,8,128]{2,1,0:T(8,128)S(1)} %add.25), channel_id=1, source_target_pairs={{0,8},{4,12},{8,0},{12,4},{1,9},{5,13},{9,1},{13,5},{2,10},{6,14},... | collective-permute-start | bytes 36872 | tf_op jit(solution)/shard_map/ppermute | solution.py:18
  59.2 2.2 %collective-permute-done.12 = f32[3,8,128]{2,1,0:T(8,128)S(1)} collective-permute-done((f32[3,8,128]{2,1,0:T(8,128)S(1)}, f32[3,8,128]{2,1,0:T(8,128)S(1)}, u32[]{:S(2)}, u32[]{:S(2)}) %collective-permute-start.12) | collective-permute-done | bytes 12320 | tf_op jit(solution)/shard_map/ppermute | solution.py:18
  61.3 0.0 collective-permute-start.13
  61.3 3.7 %collective-permute-done.13 = f32[3,8,128]{2,1,0:T(8,128)S(1)} collective-permute-done((f32[3,8,128]{2,1,0:T(8,128)S(1)}, f32[3,8,128]{2,1,0:T(8,128)S(1)}, u32[]{:S(2)}, u32[]{:S(2)}) %collective-permute-start.13) | collective-permute-done | bytes 12320 | tf_op jit(solution)/shard_map/ppermute | solution.py:18
  65.0 0.0 collective-permute-start.14
  65.0 4.6 %collective-permute-done.14 = f32[3,8,128]{2,1,0:T(8,128)S(1)} collective-permute-done((f32[3,8,128]{2,1,0:T(8,128)S(1)}, f32[3,8,128]{2,1,0:T(8,128)S(1)}, u32[]{:S(2)}, u32[]{:S(2)}) %collective-permute-start.14) | collective-permute-done | bytes 12320 | tf_op jit(solution)/shard_map/ppermute | solution.py:18
  69.6 0.6 add.28.sums
  70.2 0.0 collective-permute-done.9.there
  70.2 0.7 copy-done.3
  70.9 2.3 %shard_map.97 = (bf16[2,256,256]{2,1,0:T(8,128)(2,1)}, bf16[2,256,256]{2,1,0:T(8,128)(2,1)}) custom-call(s32[2]{0:T(128)} %block_rows.5, s32[2]{0:T(128)} %block_cols.5, f32[2]{0:T(128)} %energy.3, bf16[2,256,256]{2,1,0:T(8,128)(2,1)} %own.5, bf16[2,256,256]{2,1,0:T(8,128)(2,1)} %get-tuple-element.16.here, bf16[2,256,256]{2,1,0:T(8,128)(2,1)} %copy-done.3, ...), custom_call_target="tpu_custom_call" | custom-call | tf_op jit(solution)/shard_map/pallas_call | solution.py:151
  (12 shorter events, 0.0 us)
Async XLA Ops:
  1.6 9.0 %collective-permute-start.2 = (bf16[256,256]{1,0:T(8,128)(2,1)S(1)}, bf16[256,256]{1,0:T(8,128)(2,1)S(1)}, u32[]{:S(2)}, u32[]{:S(2)}) collective-permute-start(bf16[256,256]{1,0:T(8,128)(2,1)S(1)} %dynamic-slice_bitcast_fusion), channel_id=1, source_target_pairs={{0,3},{1,0},{2,1},{3,2},{4,7},{5,4},{6,5},{7,6},{8,11},{9,8},{10,9... | collective-permute-start | bytes 393224 | tf_op jit(solution)/shard_map/ppermute | solution.py:22
  6.7 11.2 %collective-permute-start.1 = (bf16[256,256]{1,0:T(8,128)(2,1)S(1)}, bf16[256,256]{1,0:T(8,128)(2,1)S(1)}, u32[]{:S(2)}, u32[]{:S(2)}) collective-permute-start(bf16[256,256]{1,0:T(8,128)(2,1)S(1)} %dynamic-slice_bitcast_fusion), channel_id=1, source_target_pairs={{0,2},{1,3},{2,0},{3,1},{4,6},{5,7},{6,4},{7,5},{8,10},{9,11},{10,... | collective-permute-start | bytes 393224 | tf_op jit(solution)/shard_map/ppermute | solution.py:22
  6.7 12.7 %collective-permute-start = (bf16[256,256]{1,0:T(8,128)(2,1)S(1)}, bf16[256,256]{1,0:T(8,128)(2,1)S(1)}, u32[]{:S(2)}, u32[]{:S(2)}) collective-permute-start(bf16[256,256]{1,0:T(8,128)(2,1)S(1)} %dynamic-slice_bitcast_fusion), channel_id=1, source_target_pairs={{0,1},{1,2},{2,3},{3,0},{4,5},{5,6},{6,7},{7,4},{8,9},{9,10},{10,1... | collective-permute-start | bytes 393224 | tf_op jit(solution)/shard_map/ppermute | solution.py:22
  10.6 14.9 %copy-start.4 = (bf16[256,256]{1,0:T(8,128)(2,1)}, bf16[256,256]{1,0:T(8,128)(2,1)S(1)}, u32[]{:S(2)}) copy-start(bf16[256,256]{1,0:T(8,128)(2,1)S(1)} %collective-permute-done.2.refs_2_) | copy-start | bytes 393220
  10.6 9.4 %collective-permute-start.5 = (bf16[256,256]{1,0:T(8,128)(2,1)S(1)}, bf16[256,256]{1,0:T(8,128)(2,1)S(1)}, u32[]{:S(2)}, u32[]{:S(2)}) collective-permute-start(bf16[256,256]{1,0:T(8,128)(2,1)S(1)} %collective-permute-done.2.refs_2_), channel_id=1, source_target_pairs={{0,16},{16,0},{1,17},{17,1},{2,18},{18,2},{3,19},{19,3},{4,20},{20... | collective-permute-start | bytes 393224 | tf_op jit(solution)/shard_map/ppermute | solution.py:18
  17.9 7.6 %copy-start.5 = (bf16[256,256]{1,0:T(8,128)(2,1)}, bf16[256,256]{1,0:T(8,128)(2,1)S(1)}, u32[]{:S(2)}) copy-start(bf16[256,256]{1,0:T(8,128)(2,1)S(1)} %collective-permute-done.1.refs_1_) | copy-start | bytes 393220
  17.9 6.2 %collective-permute-start.4 = (bf16[256,256]{1,0:T(8,128)(2,1)S(1)}, bf16[256,256]{1,0:T(8,128)(2,1)S(1)}, u32[]{:S(2)}, u32[]{:S(2)}) collective-permute-start(bf16[256,256]{1,0:T(8,128)(2,1)S(1)} %collective-permute-done.1.refs_1_), channel_id=1, source_target_pairs={{0,16},{16,0},{1,17},{17,1},{2,18},{18,2},{3,19},{19,3},{4,20},{20... | collective-permute-start | bytes 393224 | tf_op jit(solution)/shard_map/ppermute | solution.py:18
  19.4 6.1 %copy-start.6 = (bf16[256,256]{1,0:T(8,128)(2,1)}, bf16[256,256]{1,0:T(8,128)(2,1)S(1)}, u32[]{:S(2)}) copy-start(bf16[256,256]{1,0:T(8,128)(2,1)S(1)} %collective-permute-done.refs_0_) | copy-start | bytes 393220
  19.4 6.1 %collective-permute-start.3 = (bf16[256,256]{1,0:T(8,128)(2,1)S(1)}, bf16[256,256]{1,0:T(8,128)(2,1)S(1)}, u32[]{:S(2)}, u32[]{:S(2)}) collective-permute-start(bf16[256,256]{1,0:T(8,128)(2,1)S(1)} %collective-permute-done.refs_0_), channel_id=1, source_target_pairs={{0,16},{16,0},{1,17},{17,1},{2,18},{18,2},{3,19},{19,3},{4,20},{20... | collective-permute-start | bytes 393224 | tf_op jit(solution)/shard_map/ppermute | solution.py:18
  19.9 5.6 %copy-start.7 = (bf16[256,256]{1,0:T(8,128)(2,1)}, bf16[256,256]{1,0:T(8,128)(2,1)S(1)}, u32[]{:S(2)}) copy-start(bf16[256,256]{1,0:T(8,128)(2,1)S(1)} %collective-permute-done.5.refs_5_) | copy-start | bytes 393220
  24.1 1.4 %copy-start.8 = (bf16[256,256]{1,0:T(8,128)(2,1)}, bf16[256,256]{1,0:T(8,128)(2,1)S(1)}, u32[]{:S(2)}) copy-start(bf16[256,256]{1,0:T(8,128)(2,1)S(1)} %collective-permute-done.4.refs_4_) | copy-start | bytes 393220
  25.6 0.6 copy-start.9
  30.2 12.6 %collective-permute-start.7 = (bf16[4,256,256]{2,1,0:T(8,128)(2,1)}, bf16[4,256,256]{2,1,0:T(8,128)(2,1)S(1)}, u32[]{:S(2)}, u32[]{:S(2)}) collective-permute-start(bf16[4,256,256]{2,1,0:T(8,128)(2,1)} %shard_map.95.refs_0_), channel_id=1, source_target_pairs={{0,8},{4,12},{8,0},{12,4},{1,9},{5,13},{9,1},{13,5},{2,10},{6,14},... | collective-permute-start | bytes 1572872 | tf_op jit(solution)/shard_map/ppermute | solution.py:18
  31.7 11.1 %collective-permute-start.6 = (bf16[4,256,256]{2,1,0:T(8,128)(2,1)}, bf16[4,256,256]{2,1,0:T(8,128)(2,1)S(1)}, u32[]{:S(2)}, u32[]{:S(2)}) collective-permute-start(bf16[4,256,256]{2,1,0:T(8,128)(2,1)} %shard_map.95.refs_0_), channel_id=1, source_target_pairs={{0,4},{4,0},{8,12},{12,8},{1,5},{5,1},{9,13},{13,9},{2,6},{6,2},{1... | collective-permute-start | bytes 1572872 | tf_op jit(solution)/shard_map/ppermute | solution.py:18
  42.8 1.9 %copy-start = (bf16[4,256,256]{2,1,0:T(8,128)(2,1)}, bf16[4,256,256]{2,1,0:T(8,128)(2,1)S(1)}, u32[]{:S(2)}) copy-start(bf16[4,256,256]{2,1,0:T(8,128)(2,1)S(1)} %collective-permute-done.7.refs_2_) | copy-start | bytes 1572868
  42.8 1.9 %collective-permute-start.8 = (bf16[4,256,256]{2,1,0:T(8,128)(2,1)S(1)}, bf16[4,256,256]{2,1,0:T(8,128)(2,1)S(1)}, u32[]{:S(2)}, u32[]{:S(2)}) collective-permute-start(bf16[4,256,256]{2,1,0:T(8,128)(2,1)S(1)} %collective-permute-done.7.refs_2_), channel_id=1, source_target_pairs={{0,4},{4,0},{8,12},{12,8},{1,5},{5,1},{9,13},{13,9},{2,6},{6,2},{1... | collective-permute-start | bytes 1572872 | tf_op jit(solution)/shard_map/ppermute | solution.py:18
  42.8 1.9 %copy-start.1 = (bf16[4,256,256]{2,1,0:T(8,128)(2,1)}, bf16[4,256,256]{2,1,0:T(8,128)(2,1)S(1)}, u32[]{:S(2)}) copy-start(bf16[4,256,256]{2,1,0:T(8,128)(2,1)S(1)} %collective-permute-done.6.refs_1_) | copy-start | bytes 1572868
  44.7 0.8 %copy-start.2 = (bf16[4,256,256]{2,1,0:T(8,128)(2,1)}, bf16[4,256,256]{2,1,0:T(8,128)(2,1)S(1)}, u32[]{:S(2)}) copy-start(bf16[4,256,256]{2,1,0:T(8,128)(2,1)S(1)} %collective-permute-done.8.refs_3_) | copy-start | bytes 1572868
  50.6 3.6 %collective-permute-start.10 = (f32[8,128]{1,0:T(8,128)S(1)}, f32[8,128]{1,0:T(8,128)S(1)}, u32[]{:S(2)}, u32[]{:S(2)}) collective-permute-start(f32[8,128]{1,0:T(8,128)S(1)} %slice_bitcast_fusion), channel_id=1, source_target_pairs={{0,16},{16,0},{1,17},{17,1},{2,18},{18,2},{3,19},{19,3},{4,20},{20... | collective-permute-start | bytes 12296 | tf_op jit(solution)/shard_map/ppermute | solution.py:18
  52.1 18.1 %collective-permute-start.9 = (bf16[2,256,256]{2,1,0:T(8,128)(2,1)}, bf16[2,256,256]{2,1,0:T(8,128)(2,1)S(1)}, u32[]{:S(2)}, u32[]{:S(2)}) collective-permute-start(bf16[2,256,256]{2,1,0:T(8,128)(2,1)} %get-tuple-element.16.here), channel_id=1, source_target_pairs={{0,16},{16,0},{1,17},{17,1},{2,18},{18,2},{3,19},{19,3},{4,20},{20... | collective-permute-start | bytes 786440 | tf_op jit(solution)/shard_map/ppermute | solution.py:18
  55.5 1.4 %collective-permute-start.11 = (f32[3,8,128]{2,1,0:T(8,128)}, f32[3,8,128]{2,1,0:T(8,128)S(1)}, u32[]{:S(2)}, u32[]{:S(2)}) collective-permute-start(f32[3,8,128]{2,1,0:T(8,128)} %fusion), channel_id=1, source_target_pairs={{0,4},{4,0},{8,12},{12,8},{1,5},{5,1},{9,13},{13,9},{2,6},{6,2},{1... | collective-permute-start | bytes 36872 | tf_op jit(solution)/shard_map/ppermute | solution.py:18
  57.6 3.7 %collective-permute-start.12 = (f32[3,8,128]{2,1,0:T(8,128)S(1)}, f32[3,8,128]{2,1,0:T(8,128)S(1)}, u32[]{:S(2)}, u32[]{:S(2)}) collective-permute-start(f32[3,8,128]{2,1,0:T(8,128)S(1)} %add.25), channel_id=1, source_target_pairs={{0,8},{4,12},{8,0},{12,4},{1,9},{5,13},{9,1},{13,5},{2,10},{6,14},... | collective-permute-start | bytes 36872 | tf_op jit(solution)/shard_map/ppermute | solution.py:18
  61.3 3.7 %collective-permute-start.13 = (f32[3,8,128]{2,1,0:T(8,128)S(1)}, f32[3,8,128]{2,1,0:T(8,128)S(1)}, u32[]{:S(2)}, u32[]{:S(2)}) collective-permute-start(f32[3,8,128]{2,1,0:T(8,128)S(1)} %add.26), channel_id=1, source_target_pairs={{0,1},{1,0},{2,3},{3,2},{4,5},{5,4},{6,7},{7,6},{8,9},{9,8},{10,11... | collective-permute-start | bytes 36872 | tf_op jit(solution)/shard_map/ppermute | solution.py:18
  65.0 4.6 %collective-permute-start.14 = (f32[3,8,128]{2,1,0:T(8,128)S(1)}, f32[3,8,128]{2,1,0:T(8,128)S(1)}, u32[]{:S(2)}, u32[]{:S(2)}) collective-permute-start(f32[3,8,128]{2,1,0:T(8,128)S(1)} %add.27), channel_id=1, source_target_pairs={{0,2},{1,3},{2,0},{3,1},{4,6},{5,7},{6,4},{7,5},{8,10},{9,11},{10,... | collective-permute-start | bytes 36872 | tf_op jit(solution)/shard_map/ppermute | solution.py:18
  70.2 0.7 copy-start.3
